TPU v7x, 32 devices: a whole 2x2x4 slice. The times are simulated.
32 devices in a mesh: fsdp: 32 (over z, y, x, core), dp: 1.
Axes of the slice: x: 2, y: 2, z: 4, core: 2. Of those that a mesh axis runs over, the one named last changes fastest.
Arguments:
- inputs: bfloat16 [8192, 2560], P(('fsdp', 'dp')), may hold values from -6 to 6
- value_cotangent: bfloat16 [8192, 512], P(('fsdp', 'dp')), may hold values from -0.15625 to 0.15625
- master: float32 [2560, 4, 128], P('fsdp', None, 'dp'), may hold values from -0.125 to 0.125
- first_moment: float32 [2560, 4, 128], P('fsdp', None, 'dp'), may hold values from -6 to 6
- second_moment: float32 [2560, 4, 128], P('fsdp', None, 'dp'), may hold values from 0.25 to 4
Outputs:
- moment_one_new: float32 [2560, 4, 128], P('fsdp', None, 'dp')
- moment_two_new: float32 [2560, 4, 128], P('fsdp', None, 'dp')
- master_new: float32 [2560, 4, 128], P('fsdp', None, 'dp')
- head_blocks: bfloat16 [32, 2560, 128], P('fsdp', None, 'dp')
All inputs are finite; a program needn't handle non-finite values.
Results may differ from a plain program's by a relative error of at most 0.0018.
Values may be sent and summed in bfloat16 or wider, within the bound.
A program may use at most 64 MiB of HBM per device.

v0:
```python
import jax
import jax.numpy as jnp
from jax import lax
from jax.sharding import PartitionSpec as P

KVH = 4
HEAD = 128
STEP = 8


beta_first = 0.9
beta_second = 0.95
learn_rate = 0.001
weight_decay = 0.1
epsilon = 1e-08


def adam_update(gradient, moment_one, moment_two, weights):
    moment_one_new = beta_first * moment_one + (1.0 - beta_first) * gradient
    moment_two_new = beta_second * moment_two + (1.0 - beta_second) * gradient * gradient
    correct_one = 1.0 - beta_first**STEP
    correct_two = 1.0 - beta_second**STEP
    update = (
        moment_one_new / correct_one / (jnp.sqrt(moment_two_new / correct_two) + epsilon)
        + weight_decay * weights
    )
    return (moment_one_new, moment_two_new, weights - learn_rate * update)


def shards(inputs, value_cotangent, master, first_moment, second_moment):
    slice_width = master.shape[2]
    head_parts = []
    for head in range(KVH):
        head_cot = value_cotangent[:, head * HEAD : (head + 1) * HEAD]
        head_term = lax.dot_general(
            inputs, head_cot, (((0,), (0,)), ((), ())), preferred_element_type=jnp.float32
        )
        head_parts.append(
            lax.psum_scatter(
                head_term.astype(jnp.bfloat16), "dp", scatter_dimension=1, tiled=True
            ).astype(jnp.float32)
        )
    column_part = jnp.stack(head_parts, axis=1)
    grad_share = lax.psum_scatter(column_part, "fsdp", scatter_dimension=0, tiled=True)
    moment_one_new, moment_two_new, master_new = adam_update(
        grad_share, first_moment, second_moment, master
    )
    narrow_weight = master_new.astype(jnp.bfloat16)
    gathered = lax.all_gather(narrow_weight, "fsdp", axis=0, tiled=True)
    head_index = lax.axis_index("fsdp") % KVH
    picked = lax.dynamic_slice_in_dim(gathered, head_index, 1, 1)
    tp_block = picked.reshape(1, gathered.shape[0], slice_width)
    return (moment_one_new, moment_two_new, master_new, tp_block)


def solution(mesh):
    placed = (
        P(("fsdp", "dp"), None),
        P(("fsdp", "dp"), None),
        P("fsdp", None, "dp"),
        P("fsdp", None, "dp"),
        P("fsdp", None, "dp"),
    )
    return jax.shard_map(
        shards,
        mesh=mesh,
        in_specs=placed,
        out_specs=(
            P("fsdp", None, "dp"),
            P("fsdp", None, "dp"),
            P("fsdp", None, "dp"),
            P("fsdp", None, "dp"),
        ),
        check_vma=False,
    )
```

profile of v0, /device:TPU:11, one launch (start us, length us, event | category | flops | bytes accessed | tf_op | source)
XLA Modules:
  0.0 225.3 jit_solution(2543795695347011631)
XLA Ops:
  7.2 0.0 copy-start
  7.2 0.0 copy-start.1
  7.2 0.0 reduce-scatter.2.cloned.1.call-start
  7.2 1.3 copy-done
  8.5 1.4 fusion.3
  9.9 0.0 copy-done.1
  9.9 0.6 fusion.2
  10.5 0.6 fusion.1
  11.0 0.6 fusion
  11.6 2.7 %maximum_convert_fusion = f32[2560,4,128]{2,0,1:T(8,128)} fusion(bf16[2560,1,128]{2,0,1:T(8,128)(2,1)S(1)} %fusion.3, bf16[2560,1,128]{2,0,1:T(8,128)(2,1)S(1)} %fusion.2, bf16[2560,1,128]{2,0,1:T(8,128)(2,1)S(1)} %fusion.1, bf16[2560,1,128]{2,0,1:T(8,128)(2,1)S(1)} %fusion), kind=kLoop, calls=%fused_computation.8 | loop fusion | flops 5242880 | bytes 7864320 | tf_op jit(solution)/shard_map/stack | solution.py:43
  14.3 0.0 copy-start.2
  14.3 0.0 reduce-scatter.2.cloned.1.call-update
  14.4 0.0 all-gather.2.cloned.1.call-start
  14.4 117.1 %reduce-scatter.2.cloned.1.call-done = f32[80,4,128]{2,0,1:T(8,128)} async-done(((f32[2560,4,128]{2,0,1:T(8,128)}), f32[80,4,128]{2,0,1:T(8,128)}) %reduce-scatter.2.cloned.1.call-update) | async-done | bytes 163856 | tf_op jit(solution)/shard_map/reduce_scatter | solution.py:44
  131.5 0.0 copy-done.2
  131.5 0.0 copy-done.3
  131.5 0.0 copy-done.4
  131.6 1.7 fusion.10
  133.2 0.0 all-gather.2.cloned.1.call-update
  133.3 0.7 copy.13
  134.0 0.7 copy.14
  134.8 0.7 copy.15
  135.5 81.0 %all-gather.2.cloned.1.call-done = bf16[2560,4,128]{2,0,1:T(8,128)(2,1)} async-done(((bf16[80,4,128]{2,0,1:T(8,128)(2,1)}), bf16[2560,4,128]{2,0,1:T(8,128)(2,1)}) %all-gather.2.cloned.1.call-update) | async-done | bytes 2621456 | tf_op jit(solution)/shard_map/all_gather | solution.py:49
  216.5 2.0 dynamic-slice_bitcast_fusion
  (2 shorter events, 0.0 us)
Async XLA Ops:
  7.2 1.3 copy-start
  7.2 2.7 %copy-start.1 = (bf16[256,512]{1,0:T(8,128)(2,1)S(1)}, bf16[256,512]{1,0:T(8,128)(2,1)}, u32[]{:S(2)}) copy-start(bf16[256,512]{1,0:T(8,128)(2,1)} %param.6) | copy-start | bytes 786436
  7.2 124.3 %reduce-scatter.2.cloned.1.call-start = ((), (), s32[]{:S(2)}) async-start(), calls=%async_computation.1 | async-start | bytes 5406720 | tf_op jit(solution)/shard_map/reduce_scatter | solution.py:44
  14.3 117.2 %copy-start.2 = (f32[80,4,128]{2,1,0:T(4,128)S(1)}, f32[80,4,128]{2,1,0:T(4,128)}, u32[]{:S(2)}) copy-start(f32[80,4,128]{2,1,0:T(4,128)} %param.7) | copy-start | bytes 491524
  14.3 117.2 %copy-start.3 = (f32[80,4,128]{2,1,0:T(4,128)S(1)}, f32[80,4,128]{2,1,0:T(4,128)}, u32[]{:S(2)}) copy-start(f32[80,4,128]{2,1,0:T(4,128)} %param.9) | copy-start | bytes 491524
  14.3 117.2 %copy-start.4 = (f32[80,4,128]{2,1,0:T(4,128)S(1)}, f32[80,4,128]{2,1,0:T(4,128)}, u32[]{:S(2)}) copy-start(f32[80,4,128]{2,1,0:T(4,128)} %param.8) | copy-start | bytes 491524
  14.4 202.2 %all-gather.2.cloned.1.call-start = ((), (), s32[]{:S(2)}) async-start(), calls=%async_computation.2 | async-start | bytes 2703360 | tf_op jit(solution)/shard_map/all_gather | solution.py:49
Sparse Core Ops, SparseCore 0:
  14.5 117.0 reduce-scatter.1
  135.0 81.4 all-gather.1
where the time goes:
time: 228 us; the launch traced here: 225 us
  waiting for transfers between devices  198 us (87%)
  between operations  14.1 us (6%)
  local copies, waits for them, and re-layouts  5.43 us (2%)
  other arithmetic  4.44 us (2%)
  matrix products  3.06 us (1%)
    reduce_scatter x1, waiting for transfers between devices, shards(): lax.psum_scatter(column_part, 'fsdp', scatter_dimension=0, tiled=True)  117 us
    all_gather x1, waiting for transfers between devices, shards(): gathered = lax.all_gather(narrow_weight, 'fsdp', axis=0, tiled=True)  81 us
  transfers between devices with their start and end apart: 2, of which 2 were waited for; matrix products, arithmetic and copies ran while one was open for 1% of the time, Pallas kernels for 0%

commit v1 on v0

--- a/solution.py
+++ b/solution.py
@@ -1,10 +1,12 @@
+import functools
+
 import jax
 import jax.numpy as jnp
 from jax import lax
+from jax.experimental import pallas as pl
+from jax.experimental.pallas import tpu as pltpu
 from jax.sharding import PartitionSpec as P
 
-KVH = 4
-HEAD = 128
 STEP = 8
 
 
@@ -28,10 +30,11 @@
 
 
 def shards(inputs, value_cotangent, master, first_moment, second_moment):
-    slice_width = master.shape[2]
+    _, heads, slice_width = master.shape
+    head_size = value_cotangent.shape[1] // heads
     head_parts = []
-    for head in range(KVH):
-        head_cot = value_cotangent[:, head * HEAD : (head + 1) * HEAD]
+    for head in range(heads):
+        head_cot = value_cotangent[:, head * head_size : (head + 1) * head_size]
         head_term = lax.dot_general(
             inputs, head_cot, (((0,), (0,)), ((), ())), preferred_element_type=jnp.float32
         )
@@ -47,13 +50,197 @@
     )
     narrow_weight = master_new.astype(jnp.bfloat16)
     gathered = lax.all_gather(narrow_weight, "fsdp", axis=0, tiled=True)
-    head_index = lax.axis_index("fsdp") % KVH
+    head_index = lax.axis_index("fsdp") % heads
     picked = lax.dynamic_slice_in_dim(gathered, head_index, 1, 1)
     tp_block = picked.reshape(1, gathered.shape[0], slice_width)
     return (moment_one_new, moment_two_new, master_new, tp_block)
 
 
+def step_kernel(
+    n, x_ref, g_ref, w_ref, m_ref, v_ref, m_out, v_out, w_out, tp_out,
+    mate_x, mate_g, total, parts, arrived, narrow,
+    mate_send, mate_recv, part_send, part_recv, row_send, row_recv,
+):
+    me = lax.axis_index("fsdp")
+    core = lax.rem(me, 2)
+    chip = me // 2
+    mate = me + 1 - 2 * core
+    chips = n // 2
+    rows, heads, head_size = w_ref.shape
+    half = x_ref.shape[1] // 2
+
+    barrier = pltpu.get_barrier_semaphore()
+    for step in range(1, n):
+        pl.semaphore_signal(
+            barrier, inc=1, device_id={"fsdp": lax.rem(me + step, n)},
+            device_id_type=pl.DeviceIdType.MESH,
+        )
+    pl.semaphore_wait(barrier, n - 1)
+
+    def columns(owner):
+        return pl.ds(pl.multiple_of(owner * half, 128), half)
+
+    swap_x = pltpu.make_async_remote_copy(
+        x_ref.at[:, columns(1 - core)], mate_x, mate_send.at[0], mate_recv.at[0],
+        device_id={"fsdp": mate}, device_id_type=pl.DeviceIdType.MESH,
+    )
+    swap_g = pltpu.make_async_remote_copy(
+        g_ref, mate_g, mate_send.at[1], mate_recv.at[1],
+        device_id={"fsdp": mate}, device_id_type=pl.DeviceIdType.MESH,
+    )
+    swap_g.start()
+    swap_x.start()
+
+    def transposed_dot(left, right):
+        return lax.dot_general(
+            left, right, (((0,), (0,)), ((), ())), preferred_element_type=jnp.float32
+        )
+
+    tiles = 2
+    tile = half // tiles
+    per_tile = chips // tiles
+    for t in range(tiles):
+        own = x_ref[:, pl.ds(pl.multiple_of(core * half + t * tile, 128), tile)]
+        total[t * tile : (t + 1) * tile, :] = transposed_dot(own, g_ref[...])
+    swap_g.wait_recv()
+    swap_x.wait_recv()
+
+    def part_copy(slot):
+        return pltpu.make_async_remote_copy(
+            parts.at[pl.ds(pl.multiple_of(slot * rows, 16), rows)],
+            arrived.at[chip],
+            part_send.at[slot],
+            part_recv.at[chip],
+            device_id={"fsdp": core * chips + slot},
+            device_id_type=pl.DeviceIdType.MESH,
+        )
+
+    for t in range(tiles):
+        block = slice(t * tile, (t + 1) * tile)
+        parts[block, :] = (
+            total[block, :] + transposed_dot(mate_x[:, block], mate_g[...])
+        ).astype(jnp.bfloat16)
+        for step in range(per_tile):
+            slot = t * per_tile + lax.rem(chip + step, per_tile)
+
+            @pl.when(core * chips + slot != me)
+            def _():
+                part_copy(slot).start()
+
+    worker = me // chips
+    own_slot = lax.rem(me, chips)
+
+    @pl.when(worker == core)
+    def _():
+        arrived[chip] = parts[pl.ds(pl.multiple_of(own_slot * rows, 16), rows), :]
+
+    def wait_part(source):
+        pltpu.make_async_remote_copy(
+            parts.at[pl.ds(0, rows)], arrived.at[source], part_send.at[0],
+            part_recv.at[source], device_id={"fsdp": mate},
+            device_id_type=pl.DeviceIdType.MESH,
+        ).wait_recv()
+
+    for source in range(chips):
+        @pl.when(2 * source + worker != me)
+        def _():
+            wait_part(source)
+
+    for head in range(heads):
+        span = slice(head * head_size, (head + 1) * head_size)
+        gradient = arrived[0, :, span].astype(jnp.float32)
+        for source in range(1, chips):
+            gradient = gradient + arrived[source, :, span].astype(jnp.float32)
+        m_new, v_new, w_new = adam_update(
+            gradient, m_ref[:, head, :], v_ref[:, head, :], w_ref[:, head, :]
+        )
+        m_out[:, head, :] = m_new
+        v_out[:, head, :] = v_new
+        w_out[:, head, :] = w_new
+        narrow[head] = w_new.astype(jnp.bfloat16)
+
+    def own_rows(owner):
+        return pl.ds(pl.multiple_of(owner * rows, 16), rows)
+
+    def row_copy(target):
+        return pltpu.make_async_remote_copy(
+            narrow.at[lax.rem(target, heads)],
+            tp_out.at[0, own_rows(me)],
+            row_send.at[target],
+            row_recv.at[me],
+            device_id={"fsdp": target},
+            device_id_type=pl.DeviceIdType.MESH,
+        )
+
+    for step in range(1, n):
+        row_copy(lax.rem(me + step, n)).start()
+    tp_out[0, own_rows(me), :] = narrow[lax.rem(me, heads)]
+
+    swap_g.wait_send()
+    swap_x.wait_send()
+    for slot in range(chips):
+        @pl.when(core * chips + slot != me)
+        def _():
+            part_copy(slot).wait_send()
+    for step in range(1, n):
+        other = lax.rem(me + step, n)
+        row_copy(other).wait_send()
+        pltpu.make_async_remote_copy(
+            narrow.at[0], tp_out.at[0, own_rows(other)], row_send.at[other],
+            row_recv.at[other], device_id={"fsdp": other},
+            device_id_type=pl.DeviceIdType.MESH,
+        ).wait_recv()
+
+
+def fused(n, inputs, value_cotangent, master, first_moment, second_moment):
+    tokens, features = inputs.shape
+    width = value_cotangent.shape[1]
+    rows, heads, head_size = master.shape
+    chips = n // 2
+    state = jax.ShapeDtypeStruct(master.shape, jnp.float32)
+    vmem = pl.BlockSpec(memory_space=pltpu.VMEM)
+    return pl.pallas_call(
+        functools.partial(step_kernel, n),
+        out_shape=(
+            state, state, state,
+            jax.ShapeDtypeStruct((1, features, head_size), jnp.bfloat16),
+        ),
+        in_specs=[vmem] * 5,
+        out_specs=[vmem] * 4,
+        scratch_shapes=[
+            pltpu.VMEM((tokens, features // 2), jnp.bfloat16),
+            pltpu.VMEM((tokens, width), jnp.bfloat16),
+            pltpu.VMEM((features // 2, width), jnp.float32),
+            pltpu.VMEM((features // 2, width), jnp.bfloat16),
+            pltpu.VMEM((chips, rows, width), jnp.bfloat16),
+            pltpu.VMEM((heads, rows, head_size), jnp.bfloat16),
+            pltpu.SemaphoreType.DMA((2,)),
+            pltpu.SemaphoreType.DMA((2,)),
+            pltpu.SemaphoreType.DMA((chips,)),
+            pltpu.SemaphoreType.DMA((chips,)),
+            pltpu.SemaphoreType.DMA((n,)),
+            pltpu.SemaphoreType.DMA((n,)),
+        ],
+        compiler_params=pltpu.CompilerParams(collective_id=0, has_side_effects=True),
+    )(inputs, value_cotangent, master, first_moment, second_moment)
+
+
 def solution(mesh):
+    n = mesh.shape["fsdp"]
+
+    def body(inputs, value_cotangent, master, first_moment, second_moment):
+        rows = master.shape[0]
+        direct = (
+            mesh.shape["dp"] == 1
+            and n % 4 == 0
+            and inputs.shape[1] % 512 == 0
+            and rows % 16 == 0
+            and master.shape[2] % 128 == 0
+        )
+        if direct:
+            return fused(n, inputs, value_cotangent, master, first_moment, second_moment)
+        return shards(inputs, value_cotangent, master, first_moment, second_moment)
+
     placed = (
         P(("fsdp", "dp"), None),
         P(("fsdp", "dp"), None),
@@ -62,7 +249,7 @@
         P("fsdp", None, "dp"),
     )
     return jax.shard_map(
-        shards,
+        body,
         mesh=mesh,
         in_specs=placed,
         out_specs=(

time: 228 us -> 72.6 us (0.32)
  the two profiles are of different devices: /device:TPU:11 before, /device:TPU:21 now
where the time goes in v1:
time: 72.6 us; the launch traced here: 72.4 us
  Pallas kernels  66 us (91%)
  local copies, waits for them, and re-layouts  5.68 us (8%)
    pallas_call x1, Pallas kernels, fused(): pl.pallas_call(functools.partial(step_kernel, n), out_shape=(state, state...  66 us
    unnamed x6, local copies, waits for them, and re-layouts  5.68 us

profile of v1, /device:TPU:21, one launch (start us, length us, event | category | flops | bytes accessed | tf_op | source)
XLA Modules:
  0.0 72.4 jit_solution(17251361772703673829)
XLA Ops:
  0.6 66.0 %shard_map.84 = (f32[80,4,128]{2,1,0:T(4,128)}, f32[80,4,128]{2,1,0:T(4,128)}, f32[80,4,128]{2,1,0:T(4,128)}, bf16[1,2560,128]{2,1,0:T(8,128)(2,1)}) custom-call(bf16[256,2560]{1,0:T(8,128)(2,1)} %x_ref.1, bf16[256,512]{1,0:T(8,128)(2,1)} %g_ref.1, f32[80,4,128]{2,1,0:T(4,128)} %w_ref.1, f32[80,4,128]{2,1,0:T(4,128)} %m_ref.1, f32[80,4,128]{2,1,0:T(4,128)} %v_ref.1), custom_call_target="tpu_custom_call" | custom-call | tf_op jit(solution)/shard_map/pallas_call | solution.py:202
  66.7 0.0 copy-start
  66.7 1.7 %copy.13 = f32[80,4,128]{2,1,0:T(4,128)} copy(f32[80,4,128]{2,1,0:T(4,128)} %get-tuple-element.8) | data formatting | bytes 327680
  68.3 1.6 %copy.14 = f32[80,4,128]{2,1,0:T(4,128)} copy(f32[80,4,128]{2,1,0:T(4,128)} %get-tuple-element.9) | data formatting | bytes 327680
  69.9 1.6 %copy.15 = f32[80,4,128]{2,1,0:T(4,128)} copy(f32[80,4,128]{2,1,0:T(4,128)} %get-tuple-element.10) | data formatting | bytes 327680
  71.5 0.0 copy-done
  71.5 0.8 %copy.16 = bf16[1,2560,128]{2,1,0:T(8,128)(2,1)} copy(bf16[1,2560,128]{2,1,0:T(8,128)(2,1)S(1)} %copy-done) | data formatting | bytes 1310720
Async XLA Ops:
  66.7 4.9 %copy-start = (bf16[1,2560,128]{2,1,0:T(8,128)(2,1)S(1)}, bf16[1,2560,128]{2,1,0:T(8,128)(2,1)}, u32[]{:S(2)}) copy-start(bf16[1,2560,128]{2,1,0:T(8,128)(2,1)} %get-tuple-element.11) | copy-start | bytes 1966084

commit v2 on v0

--- a/solution.py
+++ b/solution.py
@@ -1,10 +1,12 @@
+import functools
+
 import jax
 import jax.numpy as jnp
 from jax import lax
+from jax.experimental import pallas as pl
+from jax.experimental.pallas import tpu as pltpu
 from jax.sharding import PartitionSpec as P
 
-KVH = 4
-HEAD = 128
 STEP = 8
 
 
@@ -28,10 +30,11 @@
 
 
 def shards(inputs, value_cotangent, master, first_moment, second_moment):
-    slice_width = master.shape[2]
+    _, heads, slice_width = master.shape
+    head_size = value_cotangent.shape[1] // heads
     head_parts = []
-    for head in range(KVH):
-        head_cot = value_cotangent[:, head * HEAD : (head + 1) * HEAD]
+    for head in range(heads):
+        head_cot = value_cotangent[:, head * head_size : (head + 1) * head_size]
         head_term = lax.dot_general(
             inputs, head_cot, (((0,), (0,)), ((), ())), preferred_element_type=jnp.float32
         )
@@ -47,13 +50,355 @@
     )
     narrow_weight = master_new.astype(jnp.bfloat16)
     gathered = lax.all_gather(narrow_weight, "fsdp", axis=0, tiled=True)
-    head_index = lax.axis_index("fsdp") % KVH
+    head_index = lax.axis_index("fsdp") % heads
     picked = lax.dynamic_slice_in_dim(gathered, head_index, 1, 1)
     tp_block = picked.reshape(1, gathered.shape[0], slice_width)
     return (moment_one_new, moment_two_new, master_new, tp_block)
 
 
+PLANE = 8
+
+
+def head_of(slot, heads):
+    return slot * 2 % heads + slot * 2 // heads
+
+
+def step_kernel(
+    n, x_hbm, g_hbm, w_hbm, m_hbm, v_hbm, grad_out, tp_out,
+    x_ref, g_ref, w_ref, m_ref, v_ref,
+    mate_x, mate_g, total, parts, plane_in, column_part, column_in, blocks,
+    load_sem, mate_send, mate_recv, plane_send, plane_recv,
+    column_send, column_recv, line_send, line_recv, row_send, row_recv,
+):
+    me = lax.axis_index("fsdp")
+    z = me // PLANE
+    q = lax.rem(me, PLANE)
+    spot = q // 2
+    core = lax.rem(q, 2)
+    mate = me + 1 - 2 * core
+    spots = PLANE // 2
+    depth = n // PLANE
+    layers = depth // 2
+    rows, heads, head_size = w_ref.shape
+    pair = heads // 2
+    half = x_ref.shape[1] // 2
+    tile = half // layers
+    both = 2 * rows
+    worker = z // layers
+
+    loads = [
+        pltpu.make_async_copy(source, target, load_sem.at[i])
+        for i, (source, target) in enumerate(
+            ((g_hbm, g_ref), (x_hbm, x_ref), (w_hbm, w_ref), (m_hbm, m_ref), (v_hbm, v_ref))
+        )
+    ]
+    for load in loads:
+        load.start()
+
+    def to(device):
+        return dict(device_id={"fsdp": device}, device_id_type=pl.DeviceIdType.MESH)
+
+    def plane_mate(step):
+        return z * PLANE + lax.rem(q + step, PLANE)
+
+    def layer(step):
+        return lax.rem(z + step, depth)
+
+    barrier = pltpu.get_barrier_semaphore()
+    for step in range(1, PLANE):
+        pl.semaphore_signal(barrier, inc=1, **to(plane_mate(step)))
+    for step in range(1, depth):
+        for side in range(2):
+            pl.semaphore_signal(
+                barrier, inc=1, **to(layer(step) * PLANE + 2 * spot + side)
+            )
+    loads[0].wait()
+    loads[1].wait()
+    pl.semaphore_wait(barrier, PLANE - 1 + 2 * (depth - 1))
+
+    swap_g = pltpu.make_async_remote_copy(
+        g_ref, mate_g, mate_send.at[0], mate_recv.at[0], **to(mate)
+    )
+    swap_x = pltpu.make_async_remote_copy(
+        x_ref.at[:, pl.ds(pl.multiple_of((1 - core) * half, 128), half)],
+        mate_x, mate_send.at[1], mate_recv.at[1], **to(mate)
+    )
+    swap_g.start()
+    swap_x.start()
+
+    def transposed_dot(left, right):
+        return lax.dot_general(
+            left, right, (((0,), (0,)), ((), ())), preferred_element_type=jnp.float32
+        )
+
+    def columns_of(ref, phase):
+        return jnp.concatenate(
+            [
+                ref[:, head_of(s, heads) * head_size : (head_of(s, heads) + 1) * head_size]
+                for s in range(phase * pair, (phase + 1) * pair)
+            ],
+            axis=1,
+        )
+
+    wide = pair * head_size
+    for phase in range(2):
+        right = columns_of(g_ref, phase)
+        for t in range(layers):
+            own = x_ref[:, pl.ds(pl.multiple_of(core * half + t * tile, 128), tile)]
+            total[t * tile : (t + 1) * tile, phase * wide : (phase + 1) * wide] = (
+                transposed_dot(own, right)
+            )
+    swap_g.wait_recv()
+    swap_x.wait_recv()
+
+    def of_phase(phase):
+        return pl.ds(phase * pair, pair)
+
+    def plane_copy(phase, t, step, source):
+        index = (phase * layers + t) * spots
+        target = lax.rem(spot + step, spots)
+        return pltpu.make_async_remote_copy(
+            parts.at[
+                of_phase(phase), pl.ds(pl.multiple_of(t * tile + target * both, 16), both)
+            ],
+            plane_in.at[source, of_phase(phase), pl.ds(t * both, both)],
+            plane_send.at[index + target],
+            plane_recv.at[index + source],
+            **to(z * PLANE + 2 * target + core),
+        )
+
+    for phase in range(2):
+        right = columns_of(mate_g, phase)
+        for t in range(layers):
+            block = slice(t * tile, (t + 1) * tile)
+            summed = (
+                total[block, phase * wide : (phase + 1) * wide]
+                + transposed_dot(mate_x[:, block], right)
+            ).astype(jnp.bfloat16)
+            for j in range(pair):
+                parts[phase * pair + j, block, :] = summed[
+                    :, j * head_size : (j + 1) * head_size
+                ]
+            for step in range(1, spots):
+                plane_copy(phase, t, step, spot).start()
+
+    def column_copy(phase, t, side, source):
+        index = (phase * layers + t) * 2 + side
+        return pltpu.make_async_remote_copy(
+            column_part.at[of_phase(phase), pl.ds(t * both + side * rows, rows)],
+            column_in.at[source, of_phase(phase)],
+            column_send.at[index],
+            column_recv.at[phase * depth + source],
+            **to((core * layers + t) * PLANE + 2 * spot + side),
+        )
+
+    def is_me(t, side):
+        return (core * layers + t) * PLANE + 2 * spot + side == me
+
+    def plane_sum(phase, t):
+        for step in range(1, spots):
+            plane_copy(phase, t, step, lax.rem(spot + step, spots)).wait_recv()
+        span = slice(phase * pair, (phase + 1) * pair)
+        value = parts[
+            span, pl.ds(pl.multiple_of(t * tile + spot * both, 16), both), :
+        ].astype(jnp.float32)
+        for step in range(1, spots):
+            value = value + plane_in[
+                lax.rem(spot + step, spots), span, t * both : (t + 1) * both, :
+            ].astype(jnp.float32)
+        column_part[span, t * both : (t + 1) * both, :] = value.astype(jnp.bfloat16)
+        for side in range(2):
+            @pl.when(jnp.logical_not(is_me(t, side)))
+            def _():
+                column_copy(phase, t, side, z).start()
+
+            @pl.when(is_me(t, side))
+            def _():
+                column_in[z, span] = column_part[
+                    span, t * both + side * rows : t * both + (side + 1) * rows, :
+                ]
+
+    def line_copy(phase, step, source):
+        target = layer(step)
+        return pltpu.make_async_remote_copy(
+            blocks.at[z, of_phase(phase)],
+            blocks.at[source, of_phase(phase)],
+            line_send.at[phase * depth + target],
+            line_recv.at[phase * depth + source],
+            **to(target * PLANE + q),
+        )
+
+    def rows_of(owner):
+        return pl.ds(pl.multiple_of(owner * rows, 16), rows)
+
+    def slot_of(device):
+        head = lax.rem(device, heads)
+        return lax.rem(head, 2) * pair + head // 2
+
+    def row_copy(source, target):
+        return pltpu.make_async_remote_copy(
+            blocks.at[source, slot_of(target)],
+            tp_out.at[0, rows_of(source * PLANE + q)],
+            row_send.at[source * PLANE + target],
+            row_recv.at[source * PLANE + q],
+            **to(z * PLANE + target),
+        )
+
+    def spread(phase, source):
+        for step in range(1, spots):
+            row_copy(source, 2 * lax.rem(spot + step, spots) + phase).start()
+
+        @pl.when(core != phase)
+        def _():
+            row_copy(source, 2 * spot + phase).start()
+
+        @pl.when(core == phase)
+        def _():
+            tp_out[0, rows_of(source * PLANE + q), :] = blocks[source, slot_of(me)]
+
+    def update(phase):
+        for source in range(depth):
+            @pl.when(source * PLANE + 2 * spot + worker != me)
+            def _():
+                column_copy(phase, 0, 0, source).wait_recv()
+        for s in range(phase * pair, (phase + 1) * pair):
+            head = head_of(s, heads)
+            gradient = column_in[0, s].astype(jnp.float32)
+            for source in range(1, depth):
+                gradient = gradient + column_in[source, s].astype(jnp.float32)
+            grad_out[s] = gradient
+            _, _, w_new = adam_update(
+                gradient, m_ref[:, head, :], v_ref[:, head, :], w_ref[:, head, :]
+            )
+            blocks[z, s] = w_new.astype(jnp.bfloat16)
+        for step in range(depth - 1, 0, -1):
+            line_copy(phase, step, z).start()
+        spread(phase, z)
+
+    def forward(phase):
+        for step in range(1, depth):
+            source = layer(step)
+            line_copy(phase, step, source).wait_recv()
+            spread(phase, source)
+
+    pieces = [(phase, t) for phase in range(2) for t in range(layers)]
+    for piece in pieces[: layers + 1]:
+        plane_sum(*piece)
+    for load in loads[2:]:
+        load.wait()
+    update(0)
+    for piece in pieces[layers + 1 :]:
+        plane_sum(*piece)
+    forward(0)
+    update(1)
+    forward(1)
+
+    swap_g.wait_send()
+    swap_x.wait_send()
+    for phase, t in pieces:
+        for step in range(1, spots):
+            plane_copy(phase, t, step, spot).wait_send()
+        for side in range(2):
+            @pl.when(jnp.logical_not(is_me(t, side)))
+            def _():
+                column_copy(phase, t, side, z).wait_send()
+    for phase in range(2):
+        for step in range(1, depth):
+            line_copy(phase, step, z).wait_send()
+    for source in range(depth):
+        for step in range(1, PLANE):
+            other = lax.rem(q + step, PLANE)
+            row_copy(source, other).wait_send()
+            pltpu.make_async_remote_copy(
+                blocks.at[0, 0], tp_out.at[0, rows_of(source * PLANE + other)],
+                row_send.at[0], row_recv.at[source * PLANE + other], **to(mate),
+            ).wait_recv()
+
+
+def finish_kernel(g_ref, tp_ref, w_ref, m_ref, v_ref, m_out, v_out, w_out, tp_out):
+    heads = g_ref.shape[0]
+    for s in range(heads):
+        head = head_of(s, heads)
+        m_new, v_new, w_new = adam_update(
+            g_ref[s], m_ref[:, head, :], v_ref[:, head, :], w_ref[:, head, :]
+        )
+        m_out[:, head, :] = m_new
+        v_out[:, head, :] = v_new
+        w_out[:, head, :] = w_new
+    tp_out[...] = tp_ref[...]
+
+
+def fused(n, inputs, value_cotangent, master, first_moment, second_moment):
+    tokens, features = inputs.shape
+    width = value_cotangent.shape[1]
+    rows, heads, head_size = master.shape
+    half = features // 2
+    depth = n // PLANE
+    layers = depth // 2
+    spots = PLANE // 2
+    state = jax.ShapeDtypeStruct(master.shape, jnp.float32)
+    block = jax.ShapeDtypeStruct((1, features, head_size), jnp.bfloat16)
+    vmem = pl.BlockSpec(memory_space=pltpu.VMEM)
+    narrow = jnp.bfloat16
+    gradient, gathered = pl.pallas_call(
+        functools.partial(step_kernel, n),
+        out_shape=(jax.ShapeDtypeStruct((heads, rows, head_size), jnp.float32), block),
+        in_specs=[pl.BlockSpec(memory_space=pl.ANY)] * 5,
+        out_specs=[vmem] * 2,
+        scratch_shapes=[
+            pltpu.VMEM((tokens, features), narrow),
+            pltpu.VMEM((tokens, width), narrow),
+            pltpu.VMEM(master.shape, jnp.float32),
+            pltpu.VMEM(master.shape, jnp.float32),
+            pltpu.VMEM(master.shape, jnp.float32),
+            pltpu.VMEM((tokens, half), narrow),
+            pltpu.VMEM((tokens, width), narrow),
+            pltpu.VMEM((half, width), jnp.float32),
+            pltpu.VMEM((heads, half, head_size), narrow),
+            pltpu.VMEM((spots, heads, layers * 2 * rows, head_size), narrow),
+            pltpu.VMEM((heads, layers * 2 * rows, head_size), narrow),
+            pltpu.VMEM((depth, heads, rows, head_size), narrow),
+            pltpu.VMEM((depth, heads, rows, head_size), narrow),
+            pltpu.SemaphoreType.DMA((5,)),
+            pltpu.SemaphoreType.DMA((2,)),
+            pltpu.SemaphoreType.DMA((2,)),
+            pltpu.SemaphoreType.DMA((2 * layers * spots,)),
+            pltpu.SemaphoreType.DMA((2 * layers * spots,)),
+            pltpu.SemaphoreType.DMA((2 * layers * 2,)),
+            pltpu.SemaphoreType.DMA((2 * depth,)),
+            pltpu.SemaphoreType.DMA((2 * depth,)),
+            pltpu.SemaphoreType.DMA((2 * depth,)),
+            pltpu.SemaphoreType.DMA((n,)),
+            pltpu.SemaphoreType.DMA((n,)),
+        ],
+        compiler_params=pltpu.CompilerParams(collective_id=0, has_side_effects=True),
+    )(inputs, value_cotangent, master, first_moment, second_moment)
+    return pl.pallas_call(
+        finish_kernel,
+        out_shape=(state, state, state, block),
+        in_specs=[vmem] * 5,
+        out_specs=[vmem] * 4,
+    )(gradient, gathered, master, first_moment, second_moment)
+
+
 def solution(mesh):
+    n = mesh.shape["fsdp"]
+
+    def body(inputs, value_cotangent, master, first_moment, second_moment):
+        rows = master.shape[0]
+        direct = (
+            mesh.shape["dp"] == 1
+            and n % (2 * PLANE) == 0
+            and inputs.shape[1] % (256 * (n // (2 * PLANE))) == 0
+            and rows % 16 == 0
+            and master.shape[1] % 2 == 0
+            and PLANE % master.shape[1] == 0
+            and master.shape[2] % 128 == 0
+        )
+        if direct:
+            return fused(n, inputs, value_cotangent, master, first_moment, second_moment)
+        return shards(inputs, value_cotangent, master, first_moment, second_moment)
+
     placed = (
         P(("fsdp", "dp"), None),
         P(("fsdp", "dp"), None),
@@ -62,7 +407,7 @@
         P("fsdp", None, "dp"),
     )
     return jax.shard_map(
-        shards,
+        body,
         mesh=mesh,
         in_specs=placed,
         out_specs=(

time: 228 us -> 44.1 us (0.19)
  the two profiles are of different devices: /device:TPU:11 before, /device:TPU:1 now
where the time goes in v2:
time: 44.1 us; the launch traced here: 43.9 us
  Pallas kernels  43.3 us (98%)
  between operations  0.64 us (1%)
    pallas_call x1, Pallas kernels, fused(): pl.pallas_call(functools.partial(step_kernel, n), out_shape=(jax.ShapeDty...  40.3 us
    pallas_call x1, Pallas kernels, fused(): pl.pallas_call(finish_kernel, out_shape=(state, state, state, block), in_...  2.98 us

profile of v2, /device:TPU:1, one launch (start us, length us, event | category | flops | bytes accessed | tf_op | source)
XLA Modules:
  0.0 43.9 jit_solution(3820551992539865479)
XLA Ops:
  0.6 40.3 %shard_map.84 = (f32[4,80,128]{2,1,0:T(8,128)}, bf16[1,2560,128]{2,1,0:T(8,128)(2,1)}) custom-call(bf16[256,2560]{1,0:T(8,128)(2,1)} %x_hbm.1, bf16[256,512]{1,0:T(8,128)(2,1)} %g_hbm.1, f32[80,4,128]{2,1,0:T(4,128)} %w_ref.1, f32[80,4,128]{2,1,0:T(4,128)} %m_ref.1, f32[80,4,128]{2,1,0:T(4,128)} %v_ref.1), custom_call_target="tpu_custom_call" | custom-call | tf_op jit(solution)/shard_map/pallas_call | solution.py:343
  41.0 3.0 %shard_map.85 = (f32[80,4,128]{2,1,0:T(4,128)}, f32[80,4,128]{2,1,0:T(4,128)}, f32[80,4,128]{2,1,0:T(4,128)}, bf16[1,2560,128]{2,1,0:T(8,128)(2,1)}) custom-call(f32[4,80,128]{2,1,0:T(8,128)} %get-tuple-element.6.g_ref, bf16[1,2560,128]{2,1,0:T(8,128)(2,1)} %get-tuple-element.7.tp_ref, f32[80,4,128]{2,1,0:T(4,128)} %w_ref.1, f32[80,4,128]{2,1,0:T(4,128)} %m_ref.1, ...), custom_call_target="tpu_custom_call" | custom-call | tf_op jit(solution)/shard_map/pallas_call | solution.py:376

commit v3 on v2

--- a/solution.py
+++ b/solution.py
@@ -56,15 +56,13 @@
     return (moment_one_new, moment_two_new, master_new, tp_block)
 
 
+VMEM_BYTES = 67043328
+SPARE_BYTES = 64 * 1024
 PLANE = 8
 
 
-def head_of(slot, heads):
-    return slot * 2 % heads + slot * 2 // heads
-
-
 def step_kernel(
-    n, x_hbm, g_hbm, w_hbm, m_hbm, v_hbm, grad_out, tp_out,
+    n, x_hbm, g_hbm, w_hbm, m_hbm, v_hbm, m_out, v_out, w_out, tp_out,
     x_ref, g_ref, w_ref, m_ref, v_ref,
     mate_x, mate_g, total, parts, plane_in, column_part, column_in, blocks,
     load_sem, mate_send, mate_recv, plane_send, plane_recv,
@@ -80,7 +78,6 @@
     depth = n // PLANE
     layers = depth // 2
     rows, heads, head_size = w_ref.shape
-    pair = heads // 2
     half = x_ref.shape[1] // 2
     tile = half // layers
     both = 2 * rows
@@ -131,62 +128,47 @@
             left, right, (((0,), (0,)), ((), ())), preferred_element_type=jnp.float32
         )
 
-    def columns_of(ref, phase):
-        return jnp.concatenate(
-            [
-                ref[:, head_of(s, heads) * head_size : (head_of(s, heads) + 1) * head_size]
-                for s in range(phase * pair, (phase + 1) * pair)
-            ],
-            axis=1,
-        )
-
-    wide = pair * head_size
-    for phase in range(2):
-        right = columns_of(g_ref, phase)
-        for t in range(layers):
-            own = x_ref[:, pl.ds(pl.multiple_of(core * half + t * tile, 128), tile)]
-            total[t * tile : (t + 1) * tile, phase * wide : (phase + 1) * wide] = (
-                transposed_dot(own, right)
-            )
+    def rows_of_tile(t):
+        return slice(t * tile, (t + 1) * tile)
+
+    for t in range(layers):
+        own = x_ref[:, pl.ds(pl.multiple_of(core * half + t * tile, 128), tile)]
+        total[rows_of_tile(t), :] = transposed_dot(own, g_ref[...])
     swap_g.wait_recv()
     swap_x.wait_recv()
-
-    def of_phase(phase):
-        return pl.ds(phase * pair, pair)
 
     def plane_copy(phase, t, step, source):
         index = (phase * layers + t) * spots
         target = lax.rem(spot + step, spots)
         return pltpu.make_async_remote_copy(
             parts.at[
-                of_phase(phase), pl.ds(pl.multiple_of(t * tile + target * both, 16), both)
+                phase, pl.ds(pl.multiple_of(t * tile + target * both, 16), both)
             ],
-            plane_in.at[source, of_phase(phase), pl.ds(t * both, both)],
+            plane_in.at[source, phase, pl.ds(t * both, both)],
             plane_send.at[index + target],
             plane_recv.at[index + source],
             **to(z * PLANE + 2 * target + core),
         )
 
-    for phase in range(2):
-        right = columns_of(mate_g, phase)
+    for t in range(layers):
+        block = rows_of_tile(t)
+        summed = (
+            total[block, :] + transposed_dot(mate_x[:, block], mate_g[...])
+        ).astype(jnp.bfloat16)
+        for head in range(heads):
+            parts[head, block, :] = summed[:, head * head_size : (head + 1) * head_size]
+        for step in range(1, spots):
+            plane_copy(0, t, step, spot).start()
+    for phase in range(1, heads):
         for t in range(layers):
-            block = slice(t * tile, (t + 1) * tile)
-            summed = (
-                total[block, phase * wide : (phase + 1) * wide]
-                + transposed_dot(mate_x[:, block], right)
-            ).astype(jnp.bfloat16)
-            for j in range(pair):
-                parts[phase * pair + j, block, :] = summed[
-                    :, j * head_size : (j + 1) * head_size
-                ]
             for step in range(1, spots):
                 plane_copy(phase, t, step, spot).start()
 
     def column_copy(phase, t, side, source):
         index = (phase * layers + t) * 2 + side
         return pltpu.make_async_remote_copy(
-            column_part.at[of_phase(phase), pl.ds(t * both + side * rows, rows)],
-            column_in.at[source, of_phase(phase)],
+            column_part.at[phase, pl.ds(t * both + side * rows, rows)],
+            column_in.at[source, phase],
             column_send.at[index],
             column_recv.at[phase * depth + source],
             **to((core * layers + t) * PLANE + 2 * spot + side),
@@ -198,15 +180,14 @@
     def plane_sum(phase, t):
         for step in range(1, spots):
             plane_copy(phase, t, step, lax.rem(spot + step, spots)).wait_recv()
-        span = slice(phase * pair, (phase + 1) * pair)
         value = parts[
-            span, pl.ds(pl.multiple_of(t * tile + spot * both, 16), both), :
+            phase, pl.ds(pl.multiple_of(t * tile + spot * both, 16), both), :
         ].astype(jnp.float32)
         for step in range(1, spots):
             value = value + plane_in[
-                lax.rem(spot + step, spots), span, t * both : (t + 1) * both, :
+                lax.rem(spot + step, spots), phase, t * both : (t + 1) * both, :
             ].astype(jnp.float32)
-        column_part[span, t * both : (t + 1) * both, :] = value.astype(jnp.bfloat16)
+        column_part[phase, t * both : (t + 1) * both, :] = value.astype(jnp.bfloat16)
         for side in range(2):
             @pl.when(jnp.logical_not(is_me(t, side)))
             def _():
@@ -214,15 +195,15 @@
 
             @pl.when(is_me(t, side))
             def _():
-                column_in[z, span] = column_part[
-                    span, t * both + side * rows : t * both + (side + 1) * rows, :
+                column_in[z, phase] = column_part[
+                    phase, t * both + side * rows : t * both + (side + 1) * rows, :
                 ]
 
     def line_copy(phase, step, source):
         target = layer(step)
         return pltpu.make_async_remote_copy(
-            blocks.at[z, of_phase(phase)],
-            blocks.at[source, of_phase(phase)],
+            blocks.at[z, phase],
+            blocks.at[source, phase],
             line_send.at[phase * depth + target],
             line_recv.at[phase * depth + source],
             **to(target * PLANE + q),
@@ -231,13 +212,9 @@
     def rows_of(owner):
         return pl.ds(pl.multiple_of(owner * rows, 16), rows)
 
-    def slot_of(device):
-        head = lax.rem(device, heads)
-        return lax.rem(head, 2) * pair + head // 2
-
     def row_copy(source, target):
         return pltpu.make_async_remote_copy(
-            blocks.at[source, slot_of(target)],
+            blocks.at[source, lax.rem(target, heads)],
             tp_out.at[0, rows_of(source * PLANE + q)],
             row_send.at[source * PLANE + target],
             row_recv.at[source * PLANE + q],
@@ -245,35 +222,33 @@
         )
 
     def spread(phase, source):
-        for step in range(1, spots):
-            row_copy(source, 2 * lax.rem(spot + step, spots) + phase).start()
-
-        @pl.when(core != phase)
-        def _():
-            row_copy(source, 2 * spot + phase).start()
-
-        @pl.when(core == phase)
-        def _():
-            tp_out[0, rows_of(source * PLANE + q), :] = blocks[source, slot_of(me)]
+        for target in range(phase, PLANE, heads):
+            @pl.when(target != q)
+            def _():
+                row_copy(source, target).start()
+
+            @pl.when(target == q)
+            def _():
+                tp_out[0, rows_of(source * PLANE + q), :] = blocks[source, phase]
 
     def update(phase):
         for source in range(depth):
             @pl.when(source * PLANE + 2 * spot + worker != me)
             def _():
                 column_copy(phase, 0, 0, source).wait_recv()
-        for s in range(phase * pair, (phase + 1) * pair):
-            head = head_of(s, heads)
-            gradient = column_in[0, s].astype(jnp.float32)
-            for source in range(1, depth):
-                gradient = gradient + column_in[source, s].astype(jnp.float32)
-            grad_out[s] = gradient
-            _, _, w_new = adam_update(
-                gradient, m_ref[:, head, :], v_ref[:, head, :], w_ref[:, head, :]
-            )
-            blocks[z, s] = w_new.astype(jnp.bfloat16)
+        gradient = column_in[0, phase].astype(jnp.float32)
+        for source in range(1, depth):
+            gradient = gradient + column_in[source, phase].astype(jnp.float32)
+        m_new, v_new, w_new = adam_update(
+            gradient, m_ref[:, phase, :], v_ref[:, phase, :], w_ref[:, phase, :]
+        )
+        blocks[z, phase] = w_new.astype(jnp.bfloat16)
         for step in range(depth - 1, 0, -1):
             line_copy(phase, step, z).start()
         spread(phase, z)
+        m_out[:, phase, :] = m_new
+        v_out[:, phase, :] = v_new
+        w_out[:, phase, :] = w_new
 
     def forward(phase):
         for step in range(1, depth):
@@ -281,17 +256,18 @@
             line_copy(phase, step, source).wait_recv()
             spread(phase, source)
 
-    pieces = [(phase, t) for phase in range(2) for t in range(layers)]
-    for piece in pieces[: layers + 1]:
-        plane_sum(*piece)
-    for load in loads[2:]:
-        load.wait()
-    update(0)
-    for piece in pieces[layers + 1 :]:
-        plane_sum(*piece)
-    forward(0)
-    update(1)
-    forward(1)
+    pieces = [(phase, t) for phase in range(heads) for t in range(layers)]
+    for phase in range(heads + 2):
+        if phase < heads:
+            for t in range(layers):
+                plane_sum(phase, t)
+        if phase == 1:
+            for load in loads[2:]:
+                load.wait()
+        if 0 <= phase - 1 < heads:
+            update(phase - 1)
+        if 0 <= phase - 2 < heads:
+            forward(phase - 2)
 
     swap_g.wait_send()
     swap_x.wait_send()
@@ -302,7 +278,7 @@
             @pl.when(jnp.logical_not(is_me(t, side)))
             def _():
                 column_copy(phase, t, side, z).wait_send()
-    for phase in range(2):
+    for phase in range(heads):
         for step in range(1, depth):
             line_copy(phase, step, z).wait_send()
     for source in range(depth):
@@ -315,17 +291,16 @@
             ).wait_recv()
 
 
-def finish_kernel(g_ref, tp_ref, w_ref, m_ref, v_ref, m_out, v_out, w_out, tp_out):
-    heads = g_ref.shape[0]
-    for s in range(heads):
-        head = head_of(s, heads)
-        m_new, v_new, w_new = adam_update(
-            g_ref[s], m_ref[:, head, :], v_ref[:, head, :], w_ref[:, head, :]
-        )
-        m_out[:, head, :] = m_new
-        v_out[:, head, :] = v_new
-        w_out[:, head, :] = w_new
-    tp_out[...] = tp_ref[...]
+def finish_kernel(*refs):
+    count = (len(refs) - 1) // 2
+    copies = [
+        pltpu.make_async_copy(refs[i], refs[count + i], refs[-1].at[i])
+        for i in range(count)
+    ]
+    for copy in copies:
+        copy.start()
+    for copy in copies:
+        copy.wait()
 
 
 def fused(n, inputs, value_cotangent, master, first_moment, second_moment):
@@ -338,13 +313,14 @@
     spots = PLANE // 2
     state = jax.ShapeDtypeStruct(master.shape, jnp.float32)
     block = jax.ShapeDtypeStruct((1, features, head_size), jnp.bfloat16)
+    results = 12 * master.size + 2 * block.size + SPARE_BYTES
     vmem = pl.BlockSpec(memory_space=pltpu.VMEM)
     narrow = jnp.bfloat16
-    gradient, gathered = pl.pallas_call(
+    held = pl.pallas_call(
         functools.partial(step_kernel, n),
-        out_shape=(jax.ShapeDtypeStruct((heads, rows, head_size), jnp.float32), block),
-        in_specs=[pl.BlockSpec(memory_space=pl.ANY)] * 5,
-        out_specs=[vmem] * 2,
+        out_shape=tuple(pltpu.VMEM(a.shape, a.dtype) for a in (state, state, state, block)),
+        in_specs=[pl.BlockSpec(memory_space=pltpu.HBM)] * 5,
+        out_specs=[vmem] * 4,
         scratch_shapes=[
             pltpu.VMEM((tokens, features), narrow),
             pltpu.VMEM((tokens, width), narrow),
@@ -362,23 +338,27 @@
             pltpu.SemaphoreType.DMA((5,)),
             pltpu.SemaphoreType.DMA((2,)),
             pltpu.SemaphoreType.DMA((2,)),
-            pltpu.SemaphoreType.DMA((2 * layers * spots,)),
-            pltpu.SemaphoreType.DMA((2 * layers * spots,)),
-            pltpu.SemaphoreType.DMA((2 * layers * 2,)),
-            pltpu.SemaphoreType.DMA((2 * depth,)),
-            pltpu.SemaphoreType.DMA((2 * depth,)),
-            pltpu.SemaphoreType.DMA((2 * depth,)),
+            pltpu.SemaphoreType.DMA((heads * layers * spots,)),
+            pltpu.SemaphoreType.DMA((heads * layers * spots,)),
+            pltpu.SemaphoreType.DMA((heads * layers * 2,)),
+            pltpu.SemaphoreType.DMA((heads * depth,)),
+            pltpu.SemaphoreType.DMA((heads * depth,)),
+            pltpu.SemaphoreType.DMA((heads * depth,)),
             pltpu.SemaphoreType.DMA((n,)),
             pltpu.SemaphoreType.DMA((n,)),
         ],
-        compiler_params=pltpu.CompilerParams(collective_id=0, has_side_effects=True),
+        compiler_params=pltpu.CompilerParams(
+            collective_id=0, has_side_effects=True, vmem_limit_bytes=VMEM_BYTES - results
+        ),
     )(inputs, value_cotangent, master, first_moment, second_moment)
     return pl.pallas_call(
         finish_kernel,
         out_shape=(state, state, state, block),
-        in_specs=[vmem] * 5,
-        out_specs=[vmem] * 4,
-    )(gradient, gathered, master, first_moment, second_moment)
+        in_specs=[vmem] * 4,
+        out_specs=[pl.BlockSpec(memory_space=pltpu.HBM)] * 4,
+        scratch_shapes=[pltpu.SemaphoreType.DMA((4,))],
+        compiler_params=pltpu.CompilerParams(vmem_limit_bytes=VMEM_BYTES // 2),
+    )(*held)
 
 
 def solution(mesh):
@@ -391,7 +371,6 @@
             and n % (2 * PLANE) == 0
             and inputs.shape[1] % (256 * (n // (2 * PLANE))) == 0
             and rows % 16 == 0
-            and master.shape[1] % 2 == 0
             and PLANE % master.shape[1] == 0
             and master.shape[2] % 128 == 0
         )

time: 44.1 us -> 38.8 us (0.88)
  the two profiles are of different devices: /device:TPU:1 before, /device:TPU:11 now
where the time goes in v3:
time: 38.8 us; the launch traced here: 38.7 us
  Pallas kernels  38 us (98%)
  between operations  0.64 us (2%)
    pallas_call x1, Pallas kernels, fused(): pl.pallas_call(functools.partial(step_kernel, n), out_shape=tuple((pltpu....  37 us
    pallas_call x1, Pallas kernels, fused(): pl.pallas_call(finish_kernel, out_shape=(state, state, state, block), in_...  1.04 us

profile of v3, /device:TPU:11, one launch (start us, length us, event | category | flops | bytes accessed | tf_op | source)
XLA Modules:
  0.0 38.7 jit_solution(5531567237341614605)
XLA Ops:
  0.6 37.0 %shard_map.84 = (f32[80,4,128]{2,1,0:T(4,128)S(1)}, f32[80,4,128]{2,1,0:T(4,128)S(1)}, f32[80,4,128]{2,1,0:T(4,128)S(1)}, bf16[1,2560,128]{2,1,0:T(8,128)(2,1)S(1)}) custom-call(bf16[256,2560]{1,0:T(8,128)(2,1)} %x_hbm.1, bf16[256,512]{1,0:T(8,128)(2,1)} %g_hbm.1, f32[80,4,128]{2,1,0:T(4,128)} %w_hbm.1, f32[80,4,128]{2,1,0:T(4,128)} %m_hbm.1, ...), custom_call_target="tpu_custom_call" | custom-call | tf_op jit(solution)/shard_map/pallas_call | solution.py:319
  37.6 1.0 %shard_map.85 = (f32[80,4,128]{2,1,0:T(4,128)}, f32[80,4,128]{2,1,0:T(4,128)}, f32[80,4,128]{2,1,0:T(4,128)}, bf16[1,2560,128]{2,1,0:T(8,128)(2,1)}) custom-call(f32[80,4,128]{2,1,0:T(4,128)S(1)} %get-tuple-element.8.refs_0_, f32[80,4,128]{2,1,0:T(4,128)S(1)} %get-tuple-element.9.refs_1_, f32[80,4,128]{2,1,0:T(4,128)S(1)} %get-tuple-element.10.refs_2_, ...), custom_call_target="tpu_custom_call" | custom-call | tf_op jit(solution)/shard_map/pallas_call | solution.py:354

commit v4 on v3

--- a/solution.py
+++ b/solution.py
@@ -64,7 +64,7 @@
 def step_kernel(
     n, x_hbm, g_hbm, w_hbm, m_hbm, v_hbm, m_out, v_out, w_out, tp_out,
     x_ref, g_ref, w_ref, m_ref, v_ref,
-    mate_x, mate_g, total, parts, plane_in, column_part, column_in, blocks,
+    mate_x, mate_g, total, parts, relay, plane_in, column_part, column_in, blocks,
     load_sem, mate_send, mate_recv, plane_send, plane_recv,
     column_send, column_recv, line_send, line_recv, row_send, row_recv,
 ):
@@ -116,12 +116,17 @@
     swap_g = pltpu.make_async_remote_copy(
         g_ref, mate_g, mate_send.at[0], mate_recv.at[0], **to(mate)
     )
-    swap_x = pltpu.make_async_remote_copy(
-        x_ref.at[:, pl.ds(pl.multiple_of((1 - core) * half, 128), half)],
-        mate_x, mate_send.at[1], mate_recv.at[1], **to(mate)
-    )
+    swap_x = [
+        pltpu.make_async_remote_copy(
+            x_ref.at[:, pl.ds(pl.multiple_of((1 - core) * half + t * tile, 128), tile)],
+            mate_x.at[:, pl.ds(t * tile, tile)],
+            mate_send.at[1 + t], mate_recv.at[1 + t], **to(mate)
+        )
+        for t in range(layers)
+    ]
     swap_g.start()
-    swap_x.start()
+    for swap in swap_x:
+        swap.start()
 
     def transposed_dot(left, right):
         return lax.dot_general(
@@ -135,34 +140,61 @@
         own = x_ref[:, pl.ds(pl.multiple_of(core * half + t * tile, 128), tile)]
         total[rows_of_tile(t), :] = transposed_dot(own, g_ref[...])
     swap_g.wait_recv()
-    swap_x.wait_recv()
-
-    def plane_copy(phase, t, step, source):
-        index = (phase * layers + t) * spots
-        target = lax.rem(spot + step, spots)
+
+    across_x = spot + 1 - 2 * lax.rem(spot, 2)
+    across_y = lax.rem(spot + 2, spots)
+    across_both = lax.rem(across_x + 2, spots)
+
+    def order_of(t):
+        return (across_x, across_y) if t % 2 == 0 else (across_y, across_x)
+
+    def part_rows(t, target):
+        return pl.ds(pl.multiple_of(t * tile + target * both, 16), both)
+
+    def plane_copy(phase, t, kind):
+        first, second = order_of(t)
+        piece = pl.ds(t * both, both)
+        if kind == 2:
+            source, target = relay.at[phase, piece], second
+        else:
+            owner = first if kind == 0 else across_both
+            source, target = parts.at[phase, part_rows(t, owner)], first
+        index = (phase * layers + t) * 3 + kind
         return pltpu.make_async_remote_copy(
-            parts.at[
-                phase, pl.ds(pl.multiple_of(t * tile + target * both, 16), both)
-            ],
-            plane_in.at[source, phase, pl.ds(t * both, both)],
-            plane_send.at[index + target],
-            plane_recv.at[index + source],
+            source, plane_in.at[kind, phase, piece],
+            plane_send.at[index], plane_recv.at[index],
             **to(z * PLANE + 2 * target + core),
         )
+
+    def plane_start(phase, t):
+        plane_copy(phase, t, 1).start()
+        plane_copy(phase, t, 0).start()
 
     for t in range(layers):
         block = rows_of_tile(t)
+        swap_x[t].wait_recv()
         summed = (
             total[block, :] + transposed_dot(mate_x[:, block], mate_g[...])
         ).astype(jnp.bfloat16)
         for head in range(heads):
             parts[head, block, :] = summed[:, head * head_size : (head + 1) * head_size]
-        for step in range(1, spots):
-            plane_copy(0, t, step, spot).start()
-    for phase in range(1, heads):
+        plane_start(0, t)
+    if heads > 1:
         for t in range(layers):
-            for step in range(1, spots):
-                plane_copy(phase, t, step, spot).start()
+            plane_start(1, t)
+
+    def plane_relay(phase):
+        for t in range(layers):
+            piece = slice(t * both, (t + 1) * both)
+            plane_copy(phase, t, 1).wait_recv()
+            relay[phase, piece, :] = (
+                parts[phase, part_rows(t, order_of(t)[1]), :].astype(jnp.float32)
+                + plane_in[1, phase, piece, :].astype(jnp.float32)
+            ).astype(jnp.bfloat16)
+            plane_copy(phase, t, 2).start()
+        if phase + 2 < heads:
+            for t in range(layers):
+                plane_start(phase + 2, t)
 
     def column_copy(phase, t, side, source):
         index = (phase * layers + t) * 2 + side
@@ -178,15 +210,13 @@
         return (core * layers + t) * PLANE + 2 * spot + side == me
 
     def plane_sum(phase, t):
-        for step in range(1, spots):
-            plane_copy(phase, t, step, lax.rem(spot + step, spots)).wait_recv()
-        value = parts[
-            phase, pl.ds(pl.multiple_of(t * tile + spot * both, 16), both), :
+        piece = slice(t * both, (t + 1) * both)
+        plane_copy(phase, t, 0).wait_recv()
+        value = parts[phase, part_rows(t, spot), :].astype(jnp.float32) + plane_in[
+            0, phase, piece, :
         ].astype(jnp.float32)
-        for step in range(1, spots):
-            value = value + plane_in[
-                lax.rem(spot + step, spots), phase, t * both : (t + 1) * both, :
-            ].astype(jnp.float32)
+        plane_copy(phase, t, 2).wait_recv()
+        value = value + plane_in[2, phase, piece, :].astype(jnp.float32)
         column_part[phase, t * both : (t + 1) * both, :] = value.astype(jnp.bfloat16)
         for side in range(2):
             @pl.when(jnp.logical_not(is_me(t, side)))
@@ -256,24 +286,32 @@
             line_copy(phase, step, source).wait_recv()
             spread(phase, source)
 
+    def plane_finish(phase):
+        for t in range(layers):
+            plane_sum(phase, t)
+
+    events = sorted(
+        (start + pace * phase, phase, stage)
+        for stage, (start, pace) in enumerate(
+            ((3.0, 2.3), (6.1, 2.4), (10.2, 2.4), (15.1, 2.4))
+        )
+        for phase in range(heads)
+    )
+    stages = (plane_relay, plane_finish, update, forward)
+    waiting = loads[2:]
+    for _, phase, stage in events:
+        if stages[stage] is update:
+            while waiting:
+                waiting.pop().wait()
+        stages[stage](phase)
+
     pieces = [(phase, t) for phase in range(heads) for t in range(layers)]
-    for phase in range(heads + 2):
-        if phase < heads:
-            for t in range(layers):
-                plane_sum(phase, t)
-        if phase == 1:
-            for load in loads[2:]:
-                load.wait()
-        if 0 <= phase - 1 < heads:
-            update(phase - 1)
-        if 0 <= phase - 2 < heads:
-            forward(phase - 2)
-
     swap_g.wait_send()
-    swap_x.wait_send()
+    for swap in swap_x:
+        swap.wait_send()
     for phase, t in pieces:
-        for step in range(1, spots):
-            plane_copy(phase, t, step, spot).wait_send()
+        for kind in range(3):
+            plane_copy(phase, t, kind).wait_send()
         for side in range(2):
             @pl.when(jnp.logical_not(is_me(t, side)))
             def _():
@@ -310,7 +348,6 @@
     half = features // 2
     depth = n // PLANE
     layers = depth // 2
-    spots = PLANE // 2
     state = jax.ShapeDtypeStruct(master.shape, jnp.float32)
     block = jax.ShapeDtypeStruct((1, features, head_size), jnp.bfloat16)
     results = 12 * master.size + 2 * block.size + SPARE_BYTES
@@ -331,15 +368,16 @@
             pltpu.VMEM((tokens, width), narrow),
             pltpu.VMEM((half, width), jnp.float32),
             pltpu.VMEM((heads, half, head_size), narrow),
-            pltpu.VMEM((spots, heads, layers * 2 * rows, head_size), narrow),
+            pltpu.VMEM((heads, layers * 2 * rows, head_size), narrow),
+            pltpu.VMEM((3, heads, layers * 2 * rows, head_size), narrow),
             pltpu.VMEM((heads, layers * 2 * rows, head_size), narrow),
             pltpu.VMEM((depth, heads, rows, head_size), narrow),
             pltpu.VMEM((depth, heads, rows, head_size), narrow),
             pltpu.SemaphoreType.DMA((5,)),
-            pltpu.SemaphoreType.DMA((2,)),
-            pltpu.SemaphoreType.DMA((2,)),
-            pltpu.SemaphoreType.DMA((heads * layers * spots,)),
-            pltpu.SemaphoreType.DMA((heads * layers * spots,)),
+            pltpu.SemaphoreType.DMA((1 + layers,)),
+            pltpu.SemaphoreType.DMA((1 + layers,)),
+            pltpu.SemaphoreType.DMA((heads * layers * 3,)),
+            pltpu.SemaphoreType.DMA((heads * layers * 3,)),
             pltpu.SemaphoreType.DMA((heads * layers * 2,)),
             pltpu.SemaphoreType.DMA((heads * depth,)),
             pltpu.SemaphoreType.DMA((heads * depth,)),

time: 38.8 us -> 39.7 us (1.023); the launches traced: 38.7 us -> 39.1 us
  Pallas kernels: 38 us -> 38.5 us
    pallas_call x1, Pallas kernels: 37 us -> 37.5 us  [fused(): pl.pallas_call(functools.partial(step_kernel, n), out_shape=tuple((pltpu....]
where the time goes in v4:
time: 39.7 us; the launch traced here: 39.1 us
  Pallas kernels  38.5 us (97%)
  between operations  0.64 us (2%)
    pallas_call x1, Pallas kernels, fused(): pl.pallas_call(functools.partial(step_kernel, n), out_shape=tuple((pltpu....  37.5 us
    pallas_call x1, Pallas kernels, fused(): pl.pallas_call(finish_kernel, out_shape=(state, state, state, block), in_...  1.04 us

profile of v4, /device:TPU:11, one launch (start us, length us, event | category | flops | bytes accessed | tf_op | source)
XLA Modules:
  0.0 39.1 jit_solution(8852187598264201344)
XLA Ops:
  0.6 37.5 %shard_map.84 = (f32[80,4,128]{2,1,0:T(4,128)S(1)}, f32[80,4,128]{2,1,0:T(4,128)S(1)}, f32[80,4,128]{2,1,0:T(4,128)S(1)}, bf16[1,2560,128]{2,1,0:T(8,128)(2,1)S(1)}) custom-call(bf16[256,2560]{1,0:T(8,128)(2,1)} %x_hbm.1, bf16[256,512]{1,0:T(8,128)(2,1)} %g_hbm.1, f32[80,4,128]{2,1,0:T(4,128)} %w_hbm.1, f32[80,4,128]{2,1,0:T(4,128)} %m_hbm.1, ...), custom_call_target="tpu_custom_call" | custom-call | tf_op jit(solution)/shard_map/pallas_call | solution.py:356
  38.1 1.0 %shard_map.85 = (f32[80,4,128]{2,1,0:T(4,128)}, f32[80,4,128]{2,1,0:T(4,128)}, f32[80,4,128]{2,1,0:T(4,128)}, bf16[1,2560,128]{2,1,0:T(8,128)(2,1)}) custom-call(f32[80,4,128]{2,1,0:T(4,128)S(1)} %get-tuple-element.8.refs_0_, f32[80,4,128]{2,1,0:T(4,128)S(1)} %get-tuple-element.9.refs_1_, f32[80,4,128]{2,1,0:T(4,128)S(1)} %get-tuple-element.10.refs_2_, ...), custom_call_target="tpu_custom_call" | custom-call | tf_op jit(solution)/shard_map/pallas_call | solution.py:392

commit v5 on v3

--- a/solution.py
+++ b/solution.py
@@ -102,26 +102,26 @@
         return lax.rem(z + step, depth)
 
     barrier = pltpu.get_barrier_semaphore()
-    for step in range(1, PLANE):
-        pl.semaphore_signal(barrier, inc=1, **to(plane_mate(step)))
-    for step in range(1, depth):
-        for side in range(2):
-            pl.semaphore_signal(
-                barrier, inc=1, **to(layer(step) * PLANE + 2 * spot + side)
-            )
+    for step in range(1, n):
+        pl.semaphore_signal(barrier, inc=1, **to(lax.rem(me + step, n)))
     loads[0].wait()
     loads[1].wait()
-    pl.semaphore_wait(barrier, PLANE - 1 + 2 * (depth - 1))
+    pl.semaphore_wait(barrier, n - 1)
 
     swap_g = pltpu.make_async_remote_copy(
         g_ref, mate_g, mate_send.at[0], mate_recv.at[0], **to(mate)
     )
-    swap_x = pltpu.make_async_remote_copy(
-        x_ref.at[:, pl.ds(pl.multiple_of((1 - core) * half, 128), half)],
-        mate_x, mate_send.at[1], mate_recv.at[1], **to(mate)
-    )
+    swap_x = [
+        pltpu.make_async_remote_copy(
+            x_ref.at[:, pl.ds(pl.multiple_of((1 - core) * half + t * tile, 128), tile)],
+            mate_x.at[:, pl.ds(t * tile, tile)],
+            mate_send.at[1 + t], mate_recv.at[1 + t], **to(mate)
+        )
+        for t in range(layers)
+    ]
     swap_g.start()
-    swap_x.start()
+    for swap in swap_x:
+        swap.start()
 
     def transposed_dot(left, right):
         return lax.dot_general(
@@ -135,7 +135,6 @@
         own = x_ref[:, pl.ds(pl.multiple_of(core * half + t * tile, 128), tile)]
         total[rows_of_tile(t), :] = transposed_dot(own, g_ref[...])
     swap_g.wait_recv()
-    swap_x.wait_recv()
 
     def plane_copy(phase, t, step, source):
         index = (phase * layers + t) * spots
@@ -152,6 +151,7 @@
 
     for t in range(layers):
         block = rows_of_tile(t)
+        swap_x[t].wait_recv()
         summed = (
             total[block, :] + transposed_dot(mate_x[:, block], mate_g[...])
         ).astype(jnp.bfloat16)
@@ -231,6 +231,17 @@
             def _():
                 tp_out[0, rows_of(source * PLANE + q), :] = blocks[source, phase]
 
+    last = heads - 1
+
+    def direct_copy(there, target):
+        return pltpu.make_async_remote_copy(
+            blocks.at[z, last],
+            tp_out.at[0, rows_of(me)],
+            row_send.at[there * PLANE + target],
+            row_recv.at[me],
+            **to(there * PLANE + target),
+        )
+
     def update(phase):
         for source in range(depth):
             @pl.when(source * PLANE + 2 * spot + worker != me)
@@ -243,9 +254,23 @@
             gradient, m_ref[:, phase, :], v_ref[:, phase, :], w_ref[:, phase, :]
         )
         blocks[z, phase] = w_new.astype(jnp.bfloat16)
-        for step in range(depth - 1, 0, -1):
-            line_copy(phase, step, z).start()
-        spread(phase, z)
+        if phase == last:
+            for step in range(depth - 1, -1, -1):
+                for target in range(phase, PLANE, heads):
+                    if step:
+                        direct_copy(layer(step), target).start()
+                    else:
+                        @pl.when(target != q)
+                        def _():
+                            direct_copy(z, target).start()
+
+            @pl.when(lax.rem(q, heads) == last)
+            def _():
+                tp_out[0, rows_of(me), :] = blocks[z, phase]
+        else:
+            for step in range(depth - 1, 0, -1):
+                line_copy(phase, step, z).start()
+            spread(phase, z)
         m_out[:, phase, :] = m_new
         v_out[:, phase, :] = v_new
         w_out[:, phase, :] = w_new
@@ -266,11 +291,12 @@
                 load.wait()
         if 0 <= phase - 1 < heads:
             update(phase - 1)
-        if 0 <= phase - 2 < heads:
-            forward(phase - 2)
+        if 0 <= phase - 3 < last:
+            forward(phase - 3)
 
     swap_g.wait_send()
-    swap_x.wait_send()
+    for swap in swap_x:
+        swap.wait_send()
     for phase, t in pieces:
         for step in range(1, spots):
             plane_copy(phase, t, step, spot).wait_send()
@@ -278,7 +304,7 @@
             @pl.when(jnp.logical_not(is_me(t, side)))
             def _():
                 column_copy(phase, t, side, z).wait_send()
-    for phase in range(heads):
+    for phase in range(last):
         for step in range(1, depth):
             line_copy(phase, step, z).wait_send()
     for source in range(depth):
@@ -288,6 +314,15 @@
             pltpu.make_async_remote_copy(
                 blocks.at[0, 0], tp_out.at[0, rows_of(source * PLANE + other)],
                 row_send.at[0], row_recv.at[source * PLANE + other], **to(mate),
+            ).wait_recv()
+
+    @pl.when(lax.rem(q, heads) == last)
+    def _():
+        for step in range(1, depth):
+            direct_copy(layer(step), q).wait_send()
+            pltpu.make_async_remote_copy(
+                blocks.at[0, 0], tp_out.at[0, rows_of(layer(step) * PLANE + q)],
+                row_send.at[0], row_recv.at[layer(step) * PLANE + q], **to(mate),
             ).wait_recv()
 
 
@@ -336,8 +371,8 @@
             pltpu.VMEM((depth, heads, rows, head_size), narrow),
             pltpu.VMEM((depth, heads, rows, head_size), narrow),
             pltpu.SemaphoreType.DMA((5,)),
-            pltpu.SemaphoreType.DMA((2,)),
-            pltpu.SemaphoreType.DMA((2,)),
+            pltpu.SemaphoreType.DMA((1 + layers,)),
+            pltpu.SemaphoreType.DMA((1 + layers,)),
             pltpu.SemaphoreType.DMA((heads * layers * spots,)),
             pltpu.SemaphoreType.DMA((heads * layers * spots,)),
             pltpu.SemaphoreType.DMA((heads * layers * 2,)),

time: 38.8 us -> 39.3 us (1.013)
  the two profiles are of different devices: /device:TPU:11 before, /device:TPU:2 now
where the time goes in v5:
time: 39.3 us; the launch traced here: 39.1 us
  Pallas kernels  38.5 us (98%)
  between operations  0.64 us (2%)
    pallas_call x1, Pallas kernels, fused(): pl.pallas_call(functools.partial(step_kernel, n), out_shape=tuple((pltpu....  37.4 us
    pallas_call x1, Pallas kernels, fused(): pl.pallas_call(finish_kernel, out_shape=(state, state, state, block), in_...  1.04 us

profile of v5, /device:TPU:2, one launch (start us, length us, event | category | flops | bytes accessed | tf_op | source)
XLA Modules:
  0.0 39.1 jit_solution(2500963338855524806)
XLA Ops:
  0.6 37.4 %shard_map.84 = (f32[80,4,128]{2,1,0:T(4,128)S(1)}, f32[80,4,128]{2,1,0:T(4,128)S(1)}, f32[80,4,128]{2,1,0:T(4,128)S(1)}, bf16[1,2560,128]{2,1,0:T(8,128)(2,1)S(1)}) custom-call(bf16[256,2560]{1,0:T(8,128)(2,1)} %x_hbm.1, bf16[256,512]{1,0:T(8,128)(2,1)} %g_hbm.1, f32[80,4,128]{2,1,0:T(4,128)} %w_hbm.1, f32[80,4,128]{2,1,0:T(4,128)} %m_hbm.1, ...), custom_call_target="tpu_custom_call" | custom-call | tf_op jit(solution)/shard_map/pallas_call | solution.py:354
  38.1 1.0 %shard_map.85 = (f32[80,4,128]{2,1,0:T(4,128)}, f32[80,4,128]{2,1,0:T(4,128)}, f32[80,4,128]{2,1,0:T(4,128)}, bf16[1,2560,128]{2,1,0:T(8,128)(2,1)}) custom-call(f32[80,4,128]{2,1,0:T(4,128)S(1)} %get-tuple-element.8.refs_0_, f32[80,4,128]{2,1,0:T(4,128)S(1)} %get-tuple-element.9.refs_1_, f32[80,4,128]{2,1,0:T(4,128)S(1)} %get-tuple-element.10.refs_2_, ...), custom_call_target="tpu_custom_call" | custom-call | tf_op jit(solution)/shard_map/pallas_call | solution.py:389

commit v6 on v3

--- a/solution.py
+++ b/solution.py
@@ -116,12 +116,17 @@
     swap_g = pltpu.make_async_remote_copy(
         g_ref, mate_g, mate_send.at[0], mate_recv.at[0], **to(mate)
     )
-    swap_x = pltpu.make_async_remote_copy(
-        x_ref.at[:, pl.ds(pl.multiple_of((1 - core) * half, 128), half)],
-        mate_x, mate_send.at[1], mate_recv.at[1], **to(mate)
-    )
+    swap_x = [
+        pltpu.make_async_remote_copy(
+            x_ref.at[:, pl.ds(pl.multiple_of((1 - core) * half + t * tile, 128), tile)],
+            mate_x.at[:, pl.ds(t * tile, tile)],
+            mate_send.at[1 + t], mate_recv.at[1 + t], **to(mate)
+        )
+        for t in range(layers)
+    ]
     swap_g.start()
-    swap_x.start()
+    for swap in swap_x:
+        swap.start()
 
     def transposed_dot(left, right):
         return lax.dot_general(
@@ -135,7 +140,6 @@
         own = x_ref[:, pl.ds(pl.multiple_of(core * half + t * tile, 128), tile)]
         total[rows_of_tile(t), :] = transposed_dot(own, g_ref[...])
     swap_g.wait_recv()
-    swap_x.wait_recv()
 
     def plane_copy(phase, t, step, source):
         index = (phase * layers + t) * spots
@@ -152,6 +156,7 @@
 
     for t in range(layers):
         block = rows_of_tile(t)
+        swap_x[t].wait_recv()
         summed = (
             total[block, :] + transposed_dot(mate_x[:, block], mate_g[...])
         ).astype(jnp.bfloat16)
@@ -257,7 +262,7 @@
             spread(phase, source)
 
     pieces = [(phase, t) for phase in range(heads) for t in range(layers)]
-    for phase in range(heads + 2):
+    for phase in range(heads + 3):
         if phase < heads:
             for t in range(layers):
                 plane_sum(phase, t)
@@ -266,11 +271,11 @@
                 load.wait()
         if 0 <= phase - 1 < heads:
             update(phase - 1)
-        if 0 <= phase - 2 < heads:
-            forward(phase - 2)
-
+        if 0 <= phase - 3 < heads:
+            forward(phase - 3)
     swap_g.wait_send()
-    swap_x.wait_send()
+    for swap in swap_x:
+        swap.wait_send()
     for phase, t in pieces:
         for step in range(1, spots):
             plane_copy(phase, t, step, spot).wait_send()
@@ -336,8 +341,8 @@
             pltpu.VMEM((depth, heads, rows, head_size), narrow),
             pltpu.VMEM((depth, heads, rows, head_size), narrow),
             pltpu.SemaphoreType.DMA((5,)),
-            pltpu.SemaphoreType.DMA((2,)),
-            pltpu.SemaphoreType.DMA((2,)),
+            pltpu.SemaphoreType.DMA((1 + layers,)),
+            pltpu.SemaphoreType.DMA((1 + layers,)),
             pltpu.SemaphoreType.DMA((heads * layers * spots,)),
             pltpu.SemaphoreType.DMA((heads * layers * spots,)),
             pltpu.SemaphoreType.DMA((heads * layers * 2,)),

time: 38.8 us -> 38.5 us (level)
  no operation moved by 1% of the time
where the time goes in v6:
time: 38.5 us; the launch traced here: 38.3 us
  Pallas kernels  37.7 us (98%)
  between operations  0.64 us (2%)
    pallas_call x1, Pallas kernels, fused(): pl.pallas_call(functools.partial(step_kernel, n), out_shape=tuple((pltpu....  36.6 us
    pallas_call x1, Pallas kernels, fused(): pl.pallas_call(finish_kernel, out_shape=(state, state, state, block), in_...  1.04 us

profile of v6, /device:TPU:11, one launch (start us, length us, event | category | flops | bytes accessed | tf_op | source)
XLA Modules:
  0.0 38.3 jit_solution(2097392550480713367)
XLA Ops:
  0.6 36.6 %shard_map.84 = (f32[80,4,128]{2,1,0:T(4,128)S(1)}, f32[80,4,128]{2,1,0:T(4,128)S(1)}, f32[80,4,128]{2,1,0:T(4,128)S(1)}, bf16[1,2560,128]{2,1,0:T(8,128)(2,1)S(1)}) custom-call(bf16[256,2560]{1,0:T(8,128)(2,1)} %x_hbm.1, bf16[256,512]{1,0:T(8,128)(2,1)} %g_hbm.1, f32[80,4,128]{2,1,0:T(4,128)} %w_hbm.1, f32[80,4,128]{2,1,0:T(4,128)} %m_hbm.1, ...), custom_call_target="tpu_custom_call" | custom-call | tf_op jit(solution)/shard_map/pallas_call | solution.py:324
  37.3 1.0 %shard_map.85 = (f32[80,4,128]{2,1,0:T(4,128)}, f32[80,4,128]{2,1,0:T(4,128)}, f32[80,4,128]{2,1,0:T(4,128)}, bf16[1,2560,128]{2,1,0:T(8,128)(2,1)}) custom-call(f32[80,4,128]{2,1,0:T(4,128)S(1)} %get-tuple-element.8.refs_0_, f32[80,4,128]{2,1,0:T(4,128)S(1)} %get-tuple-element.9.refs_1_, f32[80,4,128]{2,1,0:T(4,128)S(1)} %get-tuple-element.10.refs_2_, ...), custom_call_target="tpu_custom_call" | custom-call | tf_op jit(solution)/shard_map/pallas_call | solution.py:359
